TPU v7x, 512 devices: a whole 4x8x8 slice. The times are simulated.
512 devices in a mesh: bank: 32 (over y, x), zero: 16 (over z, core).
Axes of the slice: x: 4, y: 8, z: 8, core: 2. Of those that a mesh axis runs over, the one named last changes fastest.
Arguments:
- master_down: float32 [64, 1024, 2048], P('bank', None, 'zero'), may hold values from -0.25 to 0.25
- router_weight: float32 [2048, 64], P('zero', 'bank'), may hold values from -0.125 to 0.125
- router_gain: float32 [2048], P('zero'), may hold values from 0.25 to 1.75
Outputs:
- final_down: bfloat16 [64, 1024, 2048], P('bank')
- scale_down: float32 [64, 1024], P('bank')
- serve_router: bfloat16 [2048, 64], replicated
All inputs are finite; a program needn't handle non-finite values. Where the computation divides by a largest or mean magnitude, that divisor is 1e-20 or more.
Results may differ from a plain program's by a relative error of at most 0.001.
Values may be sent and summed in bfloat16 or wider, within the bound.
A program may use at most 64 MiB of HBM per device.

v0:
```python
import jax
import jax.numpy as jnp
from jax import lax
from jax.sharding import PartitionSpec as P


def copy_for_each(array, axis):
    count = lax.axis_size(axis)
    return lax.all_to_all(
        jnp.broadcast_to(array[None], (count, *array.shape)), axis, 0, 0, tiled=True
    )


def of_everyone(array, axis):
    return copy_for_each(array, axis).max(axis=0)


def joined_along(pieces, dim):
    pieces = jnp.moveaxis(pieces, 0, dim)
    shape = pieces.shape
    return pieces.reshape(*shape[:dim], shape[dim] * shape[dim + 1], *shape[dim + 2 :])


def collect(array, axis, dim):
    return joined_along(copy_for_each(array, axis), dim)


def per_device(master_down, router_weight, router_gain):
    scale_down = of_everyone(jnp.max(jnp.abs(master_down), axis=2), "zero")
    narrow_down = (master_down / jnp.expand_dims(scale_down, 2)).astype(jnp.bfloat16)
    final_down = lax.all_gather(narrow_down, "zero", axis=2, tiled=True)
    part_router = (router_weight * router_gain[:, None]).astype(jnp.bfloat16)
    row_router = lax.all_gather(part_router, "zero", axis=0, tiled=True)
    serve_router = collect(row_router, "bank", 1)
    return (final_down, scale_down, serve_router)


def solution(mesh):
    placed = (P("bank", None, "zero"), P("zero", "bank"), P("zero"))
    return jax.shard_map(
        per_device,
        mesh=mesh,
        in_specs=placed,
        out_specs=(P("bank", None, None), P("bank", None), P()),
        check_vma=False,
    )
```

profile of v0, /device:TPU:1, one launch (start us, length us, event | category | flops | bytes accessed | tf_op | source)
XLA Modules:
  0.0 114.2 jit_solution(8607611359955756124)
XLA Ops:
  7.2 0.0 all-gather.2.cloned.1.call-start
  7.2 1.6 %abs_reduce_fusion = f32[2,1024]{1,0:T(2,128)S(1)} fusion(f32[2,1024,128]{2,1,0:T(8,128)} %param.3), kind=kLoop, calls=%fused_computation.1 | loop fusion | flops 522240 | bytes 1056768 | tf_op jit(solution)/shard_map/reduce_max | solution.py:29
  8.8 20.5 %all_to_all.10 = f32[16,2,1024]{2,1,0:T(2,128)S(1)} all-to-all(f32[16,2,1024]{2,1,0:T(2,128)S(1)} %broadcast_in_dim.4), channel_id=1, replica_groups=mesh['bank'=32,'zero'=16] {'zero'}, dimensions={0} | all-to-all | bytes 262144 | tf_op jit(solution)/shard_map/all_to_all | solution.py:9
  29.3 0.1 reduce_max.19
  29.4 0.0 copy-start
  29.4 2.4 %divide_convert_fusion = bf16[2,1024,128]{2,1,0:T(8,128)(2,1)} fusion(f32[2,1024,128]{2,1,0:T(8,128)} %param.3, f32[2,1024]{1,0:T(2,128)S(1)} %reduce_max.19), kind=kLoop, calls=%fused_computation | loop fusion | flops 524288 | bytes 1581056 | tf_op jit(solution)/shard_map/convert_element_type | solution.py:30
  31.8 0.0 all-gather.2.cloned.1.call-update
  31.8 0.7 multiply_convert_fusion
  32.5 14.5 %all_gather.7 = bf16[2048,2]{0,1:T(2,128)(2,1)S(1)} all-gather(bf16[128,2]{0,1:T(2,128)(2,1)S(1)} %multiply_convert_fusion), channel_id=1, replica_groups=mesh['bank'=32,'zero'=16] {'zero'}, dimensions={0}, use_global_device_ids=true | all-gather | bytes 8704 | tf_op jit(solution)/shard_map/all_gather | solution.py:33
  46.9 0.1 broadcast_in_dim.5
  47.1 21.1 %all_to_all.11 = bf16[32,2048,2]{1,2,0:T(2,128)(2,1)S(1)} all-to-all(bf16[32,2048,2]{1,2,0:T(2,128)(2,1)S(1)} %broadcast_in_dim.5), channel_id=1, replica_groups=mesh['bank'=32,'zero'=16] {'bank'}, dimensions={0} | all-to-all | bytes 524288 | tf_op jit(solution)/shard_map/all_to_all | solution.py:9
  68.2 0.8 reshape.13
  69.0 29.9 %all-gather.2.cloned.1.call-done = bf16[2,1024,2048]{2,1,0:T(8,128)(2,1)} async-done(((bf16[2,1024,128]{2,1,0:T(8,128)(2,1)}), bf16[2,1024,2048]{2,1,0:T(8,128)(2,1)}) %all-gather.2.cloned.1.call-update) | async-done | bytes 8388624 | tf_op jit(solution)/shard_map/all_gather | solution.py:31
  98.9 8.4 %copy.9 = bf16[2,1024,2048]{2,1,0:T(8,128)(2,1)} copy(bf16[2,1024,2048]{2,1,0:T(8,128)(2,1)} %all-gather.2.cloned.1.call-done) | data formatting | bytes 16777216
  107.3 0.0 copy-done
  (1 shorter events, 0.0 us)
Async XLA Ops:
  7.2 91.7 %all-gather.2.cloned.1.call-start = ((), (), s32[]{:S(2)}) async-start(), calls=%async_computation.2 | async-start | bytes 8912896 | tf_op jit(solution)/shard_map/all_gather | solution.py:31
  29.4 77.9 %copy-start = (f32[2,1024]{1,0:T(2,128)}, f32[2,1024]{1,0:T(2,128)S(1)}, u32[]{:S(2)}) copy-start(f32[2,1024]{1,0:T(2,128)S(1)} %reduce_max.19) | copy-start | bytes 24580
Sparse Core Ops, SparseCore 0:
  31.9 66.9 all-gather.1
where the time goes:
time: 114 us
  blocking collectives  56.1 us (49%)
  waiting for transfers between devices  29.9 us (26%)
  between operations  14.1 us (12%)
  local copies, waits for them, and re-layouts  9.42 us (8%)
  other arithmetic  4.68 us (4%)
    all_to_all x2, blocking collectives, copy_for_each(): lax.all_to_all(jnp.broadcast_to(array[None], (count, *array.shape)), axis...  41.6 us
    all_gather x1, waiting for transfers between devices, per_device(): final_down = lax.all_gather(narrow_down, 'zero', axis=2, tiled=True)  29.9 us
    all_gather x1, blocking collectives, per_device(): row_router = lax.all_gather(part_router, 'zero', axis=0, tiled=True)  14.5 us
    unnamed x3, local copies, waits for them, and re-layouts  8.44 us
    convert_element_type x1, other arithmetic, per_device(): (master_down / jnp.expand_dims(scale_down, 2)).astype(jnp.bfloat16)  2.36 us
  transfers between devices with their start and end apart: 1, of which 1 were waited for; matrix products, arithmetic and copies ran while one was open for 1% of the time, Pallas kernels for 0%

commit v1 on v0

--- a/solution.py
+++ b/solution.py
@@ -2,6 +2,13 @@
 import jax.numpy as jnp
 from jax import lax
 from jax.sharding import PartitionSpec as P
+from jax.lax import all_to_all, axis_size
+
+
+def steps_all_plan(panel, lane_axis, axis_k):
+    return jnp.concatenate(
+        all_to_all(jnp.stack([panel] * axis_size(lane_axis), axis=0), lane_axis, 0, 0), axis=axis_k
+    )
 
 
 def copy_for_each(array, axis):
@@ -28,7 +35,7 @@
 def per_device(master_down, router_weight, router_gain):
     scale_down = of_everyone(jnp.max(jnp.abs(master_down), axis=2), "zero")
     narrow_down = (master_down / jnp.expand_dims(scale_down, 2)).astype(jnp.bfloat16)
-    final_down = lax.all_gather(narrow_down, "zero", axis=2, tiled=True)
+    final_down = steps_all_plan(narrow_down, "zero", 2)
     part_router = (router_weight * router_gain[:, None]).astype(jnp.bfloat16)
     row_router = lax.all_gather(part_router, "zero", axis=0, tiled=True)
     serve_router = collect(row_router, "bank", 1)

time: 114 us -> 275 us (2.41)
  waiting for transfers between devices: 29.9 us -> 193 us
  blocking collectives: 56.1 us -> 17.2 us
  starting transfers between devices: 0.04 us -> 28.9 us
  local copies, waits for them, and re-layouts: 9.42 us -> 31.1 us
  between operations: 14.1 us -> 0.67 us
    all_to_all x0 -> x3, waiting for transfers between devices: none -> 193 us  [the longest x1 183 us: steps_all_plan(): all_to_all(jnp.stack([panel] * axis_size(lane_axis), axis=0), lane_axis,...]
    all_to_all x2 -> x0, blocking collectives: 41.6 us -> none  [copy_for_each(): lax.all_to_all(jnp.broadcast_to(array[None], (count, *array.shape)), axis...]
    all_gather x1 -> x0, waiting for transfers between devices: 29.9 us -> none  [per_device(): final_down = lax.all_gather(narrow_down, 'zero', axis=2, tiled=True)]
    all_to_all x0 -> x3, starting transfers between devices: none -> 28.9 us  [the longest x2 21.5 us: copy_for_each(): lax.all_to_all(jnp.broadcast_to(array[None], (count, *array.shape)), axis...]
    all_to_all x0 -> x1, local copies, waits for them, and re-layouts: none -> 11.9 us  [steps_all_plan(): all_to_all(jnp.stack([panel] * axis_size(lane_axis), axis=0), lane_axis,...]
    another operation x0 -> x1, local copies, waits for them, and re-layouts: none -> 5.28 us  [steps_all_plan(): jnp.stack([panel] * axis_size(lane_axis), axis=0)]
    unnamed x3, local copies, waits for them, and re-layouts: 8.44 us -> 11.6 us
  transfers between devices with their start and end apart: 1 -> 3, of which waited for: 1 -> 2; matrix products, arithmetic and copies ran while one was open for 1% -> 1% of each run, Pallas kernels for 0% -> 0%
where the time goes in v1:
time: 275 us; the launch traced here: 274 us
  waiting for transfers between devices  193 us (70%)
  local copies, waits for them, and re-layouts  31.1 us (11%)
  starting transfers between devices  28.9 us (11%)
  blocking collectives  17.2 us (6%)
  other arithmetic  3.88 us (1%)
    all_to_all x1, waiting for transfers between devices, steps_all_plan(): all_to_all(jnp.stack([panel] * axis_size(lane_axis), axis=0), lane_axis,...  183 us
    all_to_all x2, starting transfers between devices, copy_for_each(): lax.all_to_all(jnp.broadcast_to(array[None], (count, *array.shape)), axis...  21.5 us
    all_gather x1, blocking collectives, per_device(): row_router = lax.all_gather(part_router, 'zero', axis=0, tiled=True)  17.2 us
    all_to_all x1, local copies, waits for them, and re-layouts, steps_all_plan(): all_to_all(jnp.stack([panel] * axis_size(lane_axis), axis=0), lane_axis,...  11.9 us
    unnamed x3, local copies, waits for them, and re-layouts  11.6 us
    all_to_all x2, waiting for transfers between devices, copy_for_each(): lax.all_to_all(jnp.broadcast_to(array[None], (count, *array.shape)), axis...  10 us
    all_to_all x1, starting transfers between devices, steps_all_plan(): all_to_all(jnp.stack([panel] * axis_size(lane_axis), axis=0), lane_axis,...  7.46 us
  transfers between devices with their start and end apart: 3, of which 2 were waited for; matrix products, arithmetic and copies ran while one was open for 1% of the time, Pallas kernels for 0%

profile of v1, /device:TPU:1, one launch (start us, length us, event | category | flops | bytes accessed | tf_op | source)
XLA Modules:
  0.0 274.4 jit_solution(10368530397778361359)
XLA Ops:
  0.6 1.6 abs_reduce_fusion
  2.2 0.7 broadcast_in_dim.4
  2.9 11.8 %all-to-all-start = ((f32[16,2,1024]{2,1,0:T(2,128)}), f32[16,2,1024]{2,1,0:T(2,128)S(1)}, u32[]{:S(2)}, u32[]{:S(2)}) async-start(f32[16,2,1024]{2,1,0:T(2,128)} %broadcast_in_dim.4), calls=%async_computation | async-start | bytes 262144 | tf_op jit(solution)/shard_map/all_to_all | solution.py:16
  14.7 0.7 multiply_convert_fusion
  15.4 17.2 %all_gather.3 = bf16[2048,2]{0,1:T(2,128)(2,1)S(1)} all-gather(bf16[128,2]{0,1:T(2,128)(2,1)S(1)} %multiply_convert_fusion), channel_id=1, replica_groups=mesh['bank'=32,'zero'=16] {'zero'}, dimensions={0}, use_global_device_ids=true | all-gather | bytes 8704 | tf_op jit(solution)/shard_map/all_gather | solution.py:40
  32.6 0.0 all-to-all-done
  32.6 0.8 broadcast_in_dim.5
  33.4 9.7 %all-to-all-start.2 = ((bf16[32,2048,2]{1,2,0:T(2,128)(2,1)}), bf16[32,2048,2]{1,2,0:T(2,128)(2,1)S(1)}, u32[]{:S(2)}, u32[]{:S(2)}) async-start(bf16[32,2048,2]{1,2,0:T(2,128)(2,1)} %broadcast_in_dim.5), calls=%async_computation.2 | async-start | bytes 524288 | tf_op jit(solution)/shard_map/all_to_all | solution.py:16
  43.1 0.1 reduce_max.19
  43.2 0.0 copy-start
  43.2 1.6 divide_convert_fusion
  44.8 10.0 %all-to-all-done.2 = bf16[32,2048,2]{1,2,0:T(2,128)(2,1)S(1)} async-done(((bf16[32,2048,2]{1,2,0:T(2,128)(2,1)}), bf16[32,2048,2]{1,2,0:T(2,128)(2,1)S(1)}, u32[]{:S(2)}, u32[]{:S(2)}) %all-to-all-start.2) | async-done | bytes 262176 | tf_op jit(solution)/shard_map/all_to_all | solution.py:16
  54.8 5.3 %stack.2 = bf16[16,2,1024,128]{3,2,1,0:T(8,128)(2,1)} broadcast(bf16[2,1024,128]{2,1,0:T(8,128)(2,1)S(1)} %divide_convert_fusion), dimensions={1,2,3} | broadcast | bytes 8912896 | tf_op jit(solution)/shard_map/stack | solution.py:10
  60.0 0.0 copy-done
  60.0 7.5 %all-to-all-start.1 = ((bf16[16,2,1024,128]{3,2,1,0:T(8,128)(2,1)}), bf16[16,2,1024,128]{3,2,1,0:T(8,128)(2,1)}, u32[]{:S(2)}, u32[]{:S(2)}) async-start(bf16[16,2,1024,128]{3,2,1,0:T(8,128)(2,1)} %stack.2), calls=%async_computation.1 | async-start | bytes 16777216 | tf_op jit(solution)/shard_map/all_to_all | solution.py:10
  67.5 0.8 reshape.23
  68.3 182.6 %all-to-all-done.1 = bf16[16,2,1024,128]{3,2,1,0:T(8,128)(2,1)} async-done(((bf16[16,2,1024,128]{3,2,1,0:T(8,128)(2,1)}), bf16[16,2,1024,128]{3,2,1,0:T(8,128)(2,1)}, u32[]{:S(2)}, u32[]{:S(2)}) %all-to-all-start.1) | async-done | bytes 8388640 | tf_op jit(solution)/shard_map/all_to_all | solution.py:10
  250.9 11.9 %copy.11 = bf16[16,2,1024,128]{2,3,0,1:T(8,128)(2,1)} copy(bf16[16,2,1024,128]{3,2,1,0:T(8,128)(2,1)} %all-to-all-done.1) | data formatting | bytes 16777216 | tf_op jit(solution)/shard_map/all_to_all | solution.py:10
  262.8 11.6 %copy.12 = bf16[2,1024,2048]{2,1,0:T(8,128)(2,1)} copy(bf16[2,1024,2048]{1,2,0:T(8,128)(2,1)} %bitcast.6) | data formatting | bytes 16777216
Async XLA Ops:
  2.9 29.7 %all-to-all-start = ((f32[16,2,1024]{2,1,0:T(2,128)}), f32[16,2,1024]{2,1,0:T(2,128)S(1)}, u32[]{:S(2)}, u32[]{:S(2)}) async-start(f32[16,2,1024]{2,1,0:T(2,128)} %broadcast_in_dim.4), calls=%async_computation | async-start | bytes 262144 | tf_op jit(solution)/shard_map/all_to_all | solution.py:16
  33.4 21.3 %all-to-all-start.2 = ((bf16[32,2048,2]{1,2,0:T(2,128)(2,1)}), bf16[32,2048,2]{1,2,0:T(2,128)(2,1)S(1)}, u32[]{:S(2)}, u32[]{:S(2)}) async-start(bf16[32,2048,2]{1,2,0:T(2,128)(2,1)} %broadcast_in_dim.5), calls=%async_computation.2 | async-start | bytes 524288 | tf_op jit(solution)/shard_map/all_to_all | solution.py:16
  43.2 16.9 %copy-start = (f32[2,1024]{1,0:T(2,128)}, f32[2,1024]{1,0:T(2,128)S(1)}, u32[]{:S(2)}) copy-start(f32[2,1024]{1,0:T(2,128)S(1)} %reduce_max.19) | copy-start | bytes 24580
  60.0 190.8 %all-to-all-start.1 = ((bf16[16,2,1024,128]{3,2,1,0:T(8,128)(2,1)}), bf16[16,2,1024,128]{3,2,1,0:T(8,128)(2,1)}, u32[]{:S(2)}, u32[]{:S(2)}) async-start(bf16[16,2,1024,128]{3,2,1,0:T(8,128)(2,1)} %stack.2), calls=%async_computation.1 | async-start | bytes 16777216 | tf_op jit(solution)/shard_map/all_to_all | solution.py:10
